TPU v7x, 32 devices: a whole 2x2x4 slice. The times are simulated.
32 devices in a mesh: rep: 1, dp: 32 (over x, y, z, core).
Axes of the slice: x: 2, y: 2, z: 4, core: 2. Of those that a mesh axis runs over, the one named last changes fastest.
Arguments:
- x: bfloat16 [32, 2048, 896], P(('rep', 'dp'))
- dy: bfloat16 [32, 2048, 896], P(('rep', 'dp'))
- w_gate: bfloat16 [2, 896, 2560], replicated
- w_up: bfloat16 [2, 896, 2560], replicated
- w_down: bfloat16 [2, 2560, 896], replicated
- m_w_gate: float32 [2, 896, 2560], P(None, 'dp')
- m_w_up: float32 [2, 896, 2560], P(None, 'dp')
- m_w_down: float32 [2, 2560, 896], P(None, 'dp')
- v_w_gate: float32 [2, 896, 2560], P(None, 'dp')
- v_w_up: float32 [2, 896, 2560], P(None, 'dp')
- v_w_down: float32 [2, 2560, 896], P(None, 'dp')
Outputs:
- output 1: bfloat16 [2, 896, 2560], P('rep')
- output 2: bfloat16 [2, 896, 2560], P('rep')
- output 3: bfloat16 [2, 2560, 896], P('rep')
- output 4: float32 [2, 896, 2560], P('rep', 'dp')
- output 5: float32 [2, 896, 2560], P('rep', 'dp')
- output 6: float32 [2, 2560, 896], P('rep', 'dp')
- output 7: float32 [2, 896, 2560], P('rep', 'dp')
- output 8: float32 [2, 896, 2560], P('rep', 'dp')
- output 9: float32 [2, 2560, 896], P('rep', 'dp')
All inputs are finite; a program needn't handle non-finite values.
Results may differ from a plain program's by a relative error of at most 0.02.
Values are sent between devices in bfloat16 or wider.
A program may use at most 2 GiB of HBM per device.

v0:
```python
import jax
import jax.numpy as jnp
from jax import lax

NAMES = ("w_gate", "w_up", "w_down")


def matmul(a, w):
    return jnp.dot(a, w, preferred_element_type=jnp.float32).astype(jnp.bfloat16)


def normed(h):
    wide = h.astype(jnp.float32)
    scale = lax.rsqrt(jnp.mean(wide**2, -1, keepdims=True) + 1e-6)
    return (wide * scale).astype(jnp.bfloat16)


def layer(h, w):
    a = normed(h)
    gate = jnp.dot(a, w["w_gate"], preferred_element_type=jnp.float32)
    up = jnp.dot(a, w["w_up"], preferred_element_type=jnp.float32)
    return h + matmul((jax.nn.silu(gate) * up).astype(jnp.bfloat16), w["w_down"])


def adamw(w, m, v, g):
    m = 0.9 * m + 0.1 * g
    v = 0.95 * v + 0.05 * g * g
    step = m * lax.rsqrt(v + 1e-8) + 0.1 * w
    return (w - 0.02 * step).astype(jnp.bfloat16), m, v


def stack(weights, h):
    for number in range(weights["w_gate"].shape[0]):
        h = layer(h, {name: w[number] for name, w in weights.items()})
    return h


def solution(mesh):
    groups = mesh.shape["rep"]

    def step(x, dy, *arrays):
        weights, m, v = (arrays[i : i + 3] for i in (0, 3, 6))
        x, dy = (t.reshape(groups, -1, *t.shape[1:]) for t in (x, dy))

        def of_a_group(x, dy):
            _, back = jax.vjp(lambda w: stack(w, x), dict(zip(NAMES, weights, strict=True)))
            by_weights = back(dy)[0]
            gradients = [by_weights[name].astype(jnp.float32) for name in NAMES]
            new = [adamw(w.astype(jnp.float32), m, v, g) for w, m, v, g in zip(weights, m, v, gradients, strict=True)]
            return tuple(one[which] for which in range(3) for one in new)

        return tuple(t.reshape(-1, *t.shape[2:]) for t in jax.vmap(of_a_group)(x, dy))

    return step
```

profile of v0, /device:TPU:25, one launch (start us, length us, event | category | flops | bytes accessed | tf_op | source)
XLA Modules:
  0.0 1796.9 jit_solution(5698237815246398384)
XLA Ops:
  19.8 14.3 fusion.173
  34.2 24.5 %fusion.150 = (bf16[1,2048,2560]{2,1,0:T(8,128)(2,1)}, f32[2048,2560]{1,0:T(8,128)}) fusion(f32[2048,2560]{1,0:T(8,128)} %fusion.173, bf16[2,896,2560]{2,1,0:T(8,128)(2,1)} %param.17, bf16[1,2048,896]{1,2,0:T(8,128)(2,1)S(1)} %fusion.157), kind=kOutput, calls=%fused_computation.189 | convolution fusion | flops 9426698240 | bytes 60686336 | tf_op jit(solution)/vmap(jvp())/dot_general | solution.py:21
  58.6 15.9 fusion.160
  78.2 18.5 %fusion.163 = f32[2048,2560]{1,0:T(8,128)} fusion(bf16[2,896,2560]{2,1,0:T(8,128)(2,1)} %param.12, bf16[1,2048,896]{1,2,0:T(8,128)(2,1)S(1)} %fusion.161), kind=kOutput, calls=%fused_computation.216 | convolution fusion | flops 9395240960 | bytes 29229056 | tf_op jit(solution)/vmap(jvp())/dot_general | solution.py:20
  96.7 24.8 %fusion.149 = (bf16[1,2048,2560]{2,1,0:T(8,128)(2,1)}, f32[2048,2560]{1,0:T(8,128)}) fusion(f32[2048,2560]{1,0:T(8,128)} %fusion.163, bf16[2,896,2560]{2,1,0:T(8,128)(2,1)} %param.17, bf16[1,2048,896]{1,2,0:T(8,128)(2,1)S(1)} %fusion.161), kind=kOutput, calls=%fused_computation.187 | convolution fusion | flops 9426698240 | bytes 60686336 | tf_op jit(solution)/vmap(jvp())/dot_general | solution.py:21
  121.5 14.6 copy.33
  136.1 191.6 %while.16 = (bf16[1,2048,2560]{1,2,0:T(8,128)(2,1)}, bf16[1,2048,896]{2,1,0:T(8,128)(2,1)}, f32[80,896]{1,0:T(8,128)S(1)}, f32[80,896]{1,0:T(8,128)}, u32[]{:T(1...) while((bf16[1,2048,2560]{1,2,0:T(8,128)(2,1)}, ...), condition=%wide.windowed_dot_general_cond_rs.4.clone, body=%wide.windowed_dot_general_body_rs.4.clone.sunk | while | flops 1177456640 | bytes 84771512 | solution.py:9
  336.0 14.6 copy.35
  350.6 27.6 %convert_multiply_fusion.2 = (bf16[1,2048,2560]{2,1,0:T(8,128)(2,1)S(1)}, bf16[1,2048,2560]{2,1,0:T(8,128)(2,1)}) fusion(f32[2048,2560]{1,0:T(8,128)} %fusion.163, f32[2048,2560]{1,0:T(8,128)} %get-tuple-element.308, bf16[2,2560,896]{2,1,0:T(8,128)(2,1)} %param.15, bf16[1,2048,896]{2,1,0:T(8,128)(2,1)} %get-tuple-element.785), kind=kOutput, calls=%fused_computation.170 | convolution fusion | flops 9479127040 | bytes 71172096 | tf_op jit(solution)/vmap(transpose(jvp()))/dot_general | solution.py:9
  378.2 18.7 %fusion.142 = bf16[2048,896]{0,1:T(8,128)(2,1)} fusion(bf16[1,2048,2560]{2,1,0:T(8,128)(2,1)} %get-tuple-element.654, bf16[2,896,2560]{2,1,0:T(8,128)(2,1)} %param.12), kind=kOutput, calls=%fused_computation.176 | convolution fusion | flops 9395240960 | bytes 18743296 | tf_op jit(solution)/vmap(transpose(jvp()))/dot_general | solution.py:20
  397.0 14.6 fusion.162
  425.4 204.3 %while.17 = (bf16[1,2048,896]{2,1,0:T(8,128)(2,1)}, bf16[1,2048,2560]{1,2,0:T(8,128)(2,1)}, f32[896,80]{0,1:T(8,128)S(1)}, f32[896,80]{0,1:T(8,128)}, u32[]{:T(1...) while((bf16[1,2048,896]{2,1,0:T(8,128)(2,1)}, ...), condition=%wide.windowed_dot_general_cond_rs.5.clone, body=%wide.windowed_dot_general_body_rs.5.clone.sunk | while | flops 1177456640 | bytes 84771512 | solution.py:9
  631.2 222.7 %while.12 = (bf16[1,2048,2560]{2,1,0:T(8,128)(2,1)}, bf16[1,2048,896]{1,2,0:T(8,128)(2,1)}, f32[2560,28]{0,1:T(8,128)S(1)}, f32[2560,28]{0,1:T(8,128)}, u32[]{:T...) while((bf16[1,2048,2560]{2,1,0:T(8,128)(2,1)}, ...), condition=%wide.windowed_dot_general_cond_rs.clone, body=%wide.windowed_dot_general_body_rs.clone.sunk | while | flops 1175752704 | bytes 38634064 | solution.py:20
  723.1 7.8 collective-permute-done.1
  855.3 31.4 %convert_multiply_fusion = (bf16[1,2048,2560]{2,1,0:T(8,128)(2,1)}, bf16[1,2048,2560]{2,1,0:T(8,128)(2,1)}) fusion(f32[2048,2560]{1,0:T(8,128)} %fusion.173, f32[2048,2560]{1,0:T(8,128)} %get-tuple-element.302, bf16[2,2560,896]{2,1,0:T(8,128)(2,1)} %param.15, bf16[1,2048,896]{1,2,0:T(8,128)(2,1)} %fusion.185), kind=kOutput, calls=%fused_computation.168 | convolution fusion | flops 9479127040 | bytes 71172096 | tf_op jit(solution)/vmap(transpose(jvp()))/dot_general | solution.py:9
  886.7 221.2 %while.13 = (bf16[1,2048,2560]{2,1,0:T(8,128)(2,1)}, bf16[1,2048,896]{1,2,0:T(8,128)(2,1)}, f32[2560,28]{0,1:T(8,128)S(1)}, f32[2560,28]{0,1:T(8,128)}, u32[]{:T...) while((bf16[1,2048,2560]{2,1,0:T(8,128)(2,1)}, ...), condition=%wide.windowed_dot_general_cond_rs.1.clone, body=%wide.windowed_dot_general_body_rs.1.clone.sunk | while | flops 1175752704 | bytes 38634064 | solution.py:20
  1107.8 219.1 %while.14 = (bf16[1,2048,2560]{2,1,0:T(8,128)(2,1)}, bf16[1,2048,896]{1,2,0:T(8,128)(2,1)}, f32[2560,28]{0,1:T(8,128)S(1)}, f32[2560,28]{0,1:T(8,128)S(1)}, u32[...) while((bf16[1,2048,2560]{2,1,0:T(8,128)(2,1)}, ...), condition=%wide.windowed_dot_general_cond_rs.2.clone, body=%wide.windowed_dot_general_body_rs.2.clone.sunk | while | flops 1175752704 | bytes 38634064 | solution.py:21
  1338.3 243.9 %while.15 = (bf16[1,2048,2560]{2,1,0:T(8,128)(2,1)}, bf16[1,2048,896]{1,2,0:T(8,128)(2,1)}, f32[2560,28]{0,1:T(8,128)S(1)}, f32[2560,28]{0,1:T(8,128)S(1)}, u32[...) while((bf16[1,2048,2560]{2,1,0:T(8,128)(2,1)}, ...), condition=%wide.windowed_dot_general_cond_rs.3.clone, body=%wide.windowed_dot_general_body_rs.3.clone.sunk | while | flops 1175752704 | bytes 38634064 | solution.py:21
  1360.2 18.8 %collective-permute-done.15 = f32[2560,28]{0,1:T(8,128)} collective-permute-done((f32[2560,28]{0,1:T(8,128)S(1)}, f32[2560,28]{0,1:T(8,128)}, u32[]{:S(2)}, u32[]{:S(2)}) %collective-permute-start.15) | collective-permute-done | bytes 286752 | tf_op jit(solution)/vmap(transpose(jvp()))/dot_general | solution.py:21
  1596.2 94.7 %all-gather.12.cloned.1.call-done = bf16[1,2,896,2560]{3,1,0,2:T(2,128)(2,1)} async-done(((bf16[1,2,28,2560]{3,1,0,2:T(2,128)(2,1)}), bf16[1,2,896,2560]{3,1,0,2:T(2,128)(2,1)}) %all-gather.12.cloned.1.call-update) | async-done | bytes 9175056 | tf_op jit(solution)/reshape | solution.py:52
  1690.8 8.7 copy.70
  1699.5 73.7 %all-gather.10.cloned.1.call-done = bf16[1,2,896,2560]{3,1,0,2:T(2,128)(2,1)} async-done(((bf16[1,2,28,2560]{3,1,0,2:T(2,128)(2,1)}), bf16[1,2,896,2560]{3,1,0,2:T(2,128)(2,1)}) %all-gather.10.cloned.1.call-update) | async-done | bytes 9175056 | tf_op jit(solution)/reshape | solution.py:52
  1773.2 8.7 copy.71
  1781.9 8.0 copy.127
  (904 shorter events, 1338.9 us)
Async XLA Ops:
  7.2 1589.0 %all-gather.14.cloned.1.call-start = ((), (), s32[]{:S(2)}) async-start(), calls=%async_computation.2 | async-start | bytes 9461760 | tf_op jit(solution)/reshape | solution.py:52
  327.7 1005.8 %collective-permute-start.28 = (f32[80,896]{1,0:T(8,128)}, f32[80,896]{1,0:T(8,128)}, u32[]{:S(2)}, u32[]{:S(2)}) collective-permute-start(f32[80,896]{1,0:T(8,128)} %get-tuple-element.45), channel_id=32, source_target_pairs={{0,1},{1,2},{2,3},{3,4},{4,5},{5,6},{6,7},{7,8},{8,9},{9,10},{10,1... | collective-permute-start | bytes 860168 | tf_op jit(solution)/vmap(transpose(jvp()))/dot_general | solution.py:9
  629.6 704.9 %collective-permute-start.29 = (f32[896,80]{0,1:T(8,128)}, f32[896,80]{0,1:T(8,128)}, u32[]{:S(2)}, u32[]{:S(2)}) collective-permute-start(f32[896,80]{0,1:T(8,128)} %get-tuple-element.47), channel_id=38, source_target_pairs={{0,1},{1,2},{2,3},{3,4},{4,5},{5,6},{6,7},{7,8},{8,9},{9,10},{10,1... | collective-permute-start | bytes 860168 | tf_op jit(solution)/vmap(transpose(jvp()))/dot_general | solution.py:9
  716.4 14.5 collective-permute-start.1
  772.7 14.0 collective-permute-start.1
  828.5 13.8 collective-permute-start.1
  854.0 728.3 %collective-permute-start.24 = (f32[2560,28]{0,1:T(8,128)}, f32[2560,28]{0,1:T(8,128)}, u32[]{:S(2)}, u32[]{:S(2)}) collective-permute-start(f32[2560,28]{0,1:T(8,128)} %get-tuple-element.37), channel_id=6, source_target_pairs={{0,1},{1,2},{2,3},{3,4},{4,5},{5,6},{6,7},{7,8},{8,9},{9,10},{10,1... | collective-permute-start | bytes 860168 | tf_op jit(solution)/vmap(transpose(jvp()))/dot_general | solution.py:20
  971.0 13.8 collective-permute-start.5
  1026.7 13.8 collective-permute-start.5
  1082.3 13.8 collective-permute-start.5
  1135.4 14.0 collective-permute-start.9
  1189.9 13.8 collective-permute-start.9
  1217.3 13.9 collective-permute-start.9
  1272.2 13.9 collective-permute-start.9
  1327.0 256.3 %collective-permute-start.25 = (f32[2560,28]{0,1:T(8,128)}, f32[2560,28]{0,1:T(8,128)}, u32[]{:S(2)}, u32[]{:S(2)}) collective-permute-start(f32[2560,28]{0,1:T(8,128)} %get-tuple-element.39), channel_id=12, source_target_pairs={{0,1},{1,2},{2,3},{3,4},{4,5},{5,6},{6,7},{7,8},{8,9},{9,10},{10,1... | collective-permute-start | bytes 860168 | tf_op jit(solution)/vmap(transpose(jvp()))/dot_general | solution.py:20
  1327.1 257.3 %collective-permute-start.26 = (f32[2560,28]{0,1:T(8,128)S(1)}, f32[2560,28]{0,1:T(8,128)}, u32[]{:S(2)}, u32[]{:S(2)}) collective-permute-start(f32[2560,28]{0,1:T(8,128)S(1)} %get-tuple-element.41), channel_id=19, source_target_pairs={{0,1},{1,2},{2,3},{3,4},{4,5},{5,6},{6,7},{7,8},{8,9},{9,10},{10,1... | collective-permute-start | bytes 860168 | tf_op jit(solution)/vmap(transpose(jvp()))/dot_general | solution.py:21
  1338.2 352.6 %all-gather.12.cloned.1.call-start = ((), (), s32[]{:S(2)}) async-start(), calls=%async_computation.1 | async-start | bytes 9461760 | tf_op jit(solution)/reshape | solution.py:52
  1353.4 25.6 %collective-permute-start.15 = (f32[2560,28]{0,1:T(8,128)S(1)}, f32[2560,28]{0,1:T(8,128)}, u32[]{:S(2)}, u32[]{:S(2)}) collective-permute-start(f32[2560,28]{0,1:T(8,128)S(1)} %get-tuple-element.525), channel_id=23, source_target_pairs={{0,31},{1,0},{2,1},{3,2},{4,3},{5,4},{6,5},{7,6},{8,7},{9,8},{10,9... | collective-permute-start | bytes 860168 | tf_op jit(solution)/vmap(transpose(jvp()))/dot_general | solution.py:21
  1380.2 18.7 %collective-permute-start.13 = (f32[2560,28]{0,1:T(8,128)S(1)}, f32[2560,28]{0,1:T(8,128)S(1)}, u32[]{:S(2)}, u32[]{:S(2)}) collective-permute-start(f32[2560,28]{0,1:T(8,128)S(1)} %broadcast_select_fusion.31), channel_id=21, source_target_pairs={{0,31},{1,0},{2,1},{3,2},{4,3},{5,4},{6,5},{7,6},{8,7},{9,8},{10,9... | collective-permute-start | bytes 860168 | tf_op jit(solution)/vmap(transpose(jvp()))/dot_general | solution.py:21
  1414.5 14.3 collective-permute-start.12
  1414.6 17.9 collective-permute-start.13
  1434.8 15.3 collective-permute-start.15
  1554.1 14.0 collective-permute-start.13
  1590.1 183.1 %all-gather.10.cloned.1.call-start = ((), (), s32[]{:S(2)}) async-start(), calls=%async_computation | async-start | bytes 9461760 | tf_op jit(solution)/reshape | solution.py:52
  (258 other events, 3287.5 us)
Sparse Core Ops, SparseCore 0:
  1338.4 110.1 all-gather.13
  1590.2 100.5 all-gather.11
  1694.3 78.9 all-gather.9
where the time goes:
time: 1810 us; the launch traced here: 1800 us
  waiting for transfers between devices  823 us (45%)
  matrix products  645 us (36%)
  starting transfers between devices  127 us (7%)
  other arithmetic  103 us (6%)
  local copies, waits for them, and re-layouts  80.7 us (4%)
    dot_general x35, matrix products, layer(): up = jnp.dot(a, w['w_up'], preferred_element_type=jnp.float32)  258 us
    dot_general x66, waiting for transfers between devices, matmul(): jnp.dot(a, w, preferred_element_type=jnp.float32).astype(jnp.bfloat16)  257 us
    dot_general x35, matrix products, layer(): gate = jnp.dot(a, w['w_gate'], preferred_element_type=jnp.float32)  246 us
    dot_general x66, waiting for transfers between devices, layer(): up = jnp.dot(a, w['w_up'], preferred_element_type=jnp.float32)  221 us
    dot_general x66, waiting for transfers between devices, layer(): gate = jnp.dot(a, w['w_gate'], preferred_element_type=jnp.float32)  176 us
    reshape x3, waiting for transfers between devices, step(): t.reshape(-1, *t.shape[2:])  168 us
    dot_general x35, matrix products, matmul(): jnp.dot(a, w, preferred_element_type=jnp.float32).astype(jnp.bfloat16)  141 us
    unnamed x44, local copies, waits for them, and re-layouts  61 us
  transfers between devices with their start and end apart: 201, of which 188 were waited for; matrix products, arithmetic and copies ran while one was open for 37% of the time, Pallas kernels for 0%

commit v1 on v0

v1 whole, which is shorter than its diff:
```python
import functools

import jax
import jax.numpy as jnp
from jax import lax
from jax.experimental import pallas as pl
from jax.experimental.pallas import tpu as pltpu
from jax.sharding import PartitionSpec as P

F32, BF = jnp.float32, jnp.bfloat16
MESH = pl.DeviceIdType.MESH
WIDE, TALL = (32, 2560), (80, 896)


def dot(a, b, ca, cb):
    return lax.dot_general(a, b, (((ca,), (cb,)), ((), ())), preferred_element_type=F32)


def normed(h):
    wide = h.astype(F32)
    scale = lax.rsqrt(jnp.mean(wide**2, -1, keepdims=True) + 1e-6)
    return (wide * scale).astype(BF), scale


def spread():
    f, c = lax.broadcasted_iota(jnp.int32, (896, 1024), 0), lax.broadcasted_iota(jnp.int32, (896, 1024), 1)
    return (32 * (f // 28) + f % 28 == c).astype(BF)


def act_back(dp, g, u):
    s = jax.nn.sigmoid(g)
    dp = dp.astype(F32)
    return (dp * u * (s * (1 + g * (1 - s)))).astype(BF), (dp * g * s).astype(BF)


def gradients(x, dy, wg, wu, wd):
    place = spread()
    a0, _ = normed(x)
    g0, u0 = dot(a0, wg[0], 1, 0), dot(a0, wu[0], 1, 0)
    p0 = (jax.nn.silu(g0) * u0).astype(BF)
    h1 = x + dot(p0, wd[0], 1, 0).astype(BF)
    a1, s1 = normed(h1)
    g1, u1 = dot(a1, wg[1], 1, 0), dot(a1, wu[1], 1, 0)
    p1 = (jax.nn.silu(g1) * u1).astype(BF)
    dwd1 = dot(p1, dy, 0, 0).astype(BF)
    dg1, du1 = act_back(dot(dy, wd[1], 1, 1).astype(BF), g1, u1)
    b1 = dot(a1, place, 1, 0).astype(BF)
    dwg1, dwu1 = dot(b1, dg1, 0, 0).astype(BF), dot(b1, du1, 0, 0).astype(BF)
    da1 = dot(dg1, wg[1], 1, 1) + dot(du1, wu[1], 1, 1)
    unit = h1.astype(F32) * s1
    dh1 = dy + (s1 * (da1 - unit * jnp.mean(da1 * unit, -1, keepdims=True))).astype(BF)
    dwd0 = dot(p0, dh1, 0, 0).astype(BF)
    dg0, du0 = act_back(dot(dh1, wd[0], 1, 1).astype(BF), g0, u0)
    b0 = dot(a0, place, 1, 0).astype(BF)
    dwg0, dwu0 = dot(b0, dg0, 0, 0).astype(BF), dot(b0, du0, 0, 0).astype(BF)
    return dwd1, dwg1, dwu1, dwd0, dwg0, dwu0


CHUNKS = [(TALL, 2, 1), (WIDE, 0, 1), (WIDE, 1, 1), (TALL, 2, 0), (WIDE, 0, 0), (WIDE, 1, 0)]


def exchange(*refs):
    n = len(CHUNKS)
    grads, ws, ms, vs = refs[:n], refs[n : n + 3], refs[n + 3 : n + 6], refs[n + 6 : n + 9]
    outs, mo, vo = refs[n + 9 : 2 * n + 9], refs[2 * n + 9 : 2 * n + 12], refs[2 * n + 12 : 2 * n + 15]
    scratch = refs[2 * n + 15 :]
    own, r0, r1, r2, r3, new = (scratch[i * n : (i + 1) * n] for i in range(6))
    local_sem, send_sem, recv_sem = scratch[6 * n :]

    me = lax.axis_index("dp")
    c, z, y, x = me % 2, (me // 2) % 4, (me // 8) % 2, me // 16
    core, px, py = me + 1 - 2 * c, me + 16 - 32 * x, me + 8 - 16 * y
    pz = [me + 2 * ((z + d) % 4 - z) for d in (1, 2, 3)]

    barrier = pltpu.get_barrier_semaphore()
    for peer in (core, px, py, *pz):
        pl.semaphore_signal(barrier, inc=1, device_id={"dp": peer}, device_id_type=MESH)
    pl.semaphore_wait(barrier, 6)

    def remote(k, slot, src, dst, peer):
        return pltpu.make_async_remote_copy(
            src_ref=src, dst_ref=dst, send_sem=send_sem.at[k, slot], recv_sem=recv_sem.at[k, slot],
            device_id={"dp": peer}, device_id_type=MESH,
        )

    def rows(k, blocks, body):
        per = CHUNKS[k][0][0] // 16

        def step(i, _):
            body(i // per, pl.ds(pl.multiple_of(i % per * 16, 16), 16))
            return 0

        lax.fori_loop(0, blocks * per, step, 0)

    def wide(ref, *at):
        return ref[at].astype(F32)

    sent = []

    def go(copy):
        copy.start()
        sent.append(copy)
        return copy

    stages = [{} for _ in range(n)]
    for k in range(n):
        stages[k]["own"] = pltpu.make_async_copy(grads[k].at[:, :, :, :, c], own[k], local_sem.at[k, 0])
        stages[k]["own"].start()
        stages[k]["core"] = go(remote(k, 0, grads[k].at[:, :, :, :, 1 - c], r0[k], core))

    for k in range(n):
        stages[k]["own"].wait()
        stages[k]["core"].wait_recv()

        def first(i, r, k=k):
            q, zz = i // 2, i % 2
            at = (1 - x, q, 0, zz, r)
            r0[k][at] = (wide(r0[k], *at) + wide(own[k], *at)).astype(BF)

        rows(k, 4, first)
        stages[k]["a1"] = go(remote(k, 1, r0[k].at[1 - x, :, 0], r1[k].at[0], px))

        def second(i, r, k=k):
            q, zz = i // 2, i % 2
            at = (q, 1 - y, 1, zz, r)
            r0[k][at] = (wide(r0[k], *at) + wide(own[k], *at)).astype(BF)

        rows(k, 4, second)
        stages[k]["b1"] = go(remote(k, 2, r0[k].at[:, 1 - y, 1], r1[k].at[1], py))

    for k in range(n):
        stages[k]["a1"].wait_recv()

        def first(zz, r, k=k):
            at = (x, 1 - y, 0, zz, r)
            to = (0, 1 - y, zz, r)
            r1[k][to] = (wide(r1[k], *to) + (wide(r0[k], *at) + wide(own[k], *at))).astype(BF)

        rows(k, 2, first)
        stages[k]["a2"] = go(remote(k, 3, r1[k].at[0, 1 - y], r2[k].at[0], py))
        stages[k]["b1"].wait_recv()

        def second(zz, r, k=k):
            at = (1 - x, y, 1, zz, r)
            to = (1, 1 - x, zz, r)
            r1[k][to] = (wide(r1[k], *to) + (wide(r0[k], *at) + wide(own[k], *at))).astype(BF)

        rows(k, 2, second)
        stages[k]["b2"] = go(remote(k, 4, r1[k].at[1, 1 - x], r2[k].at[1], px))

    def so_far(k, h, zz, r):
        at = (x, y, h, zz, r)
        return wide(r2[k], h, zz, r) + wide(r1[k], h, y * (1 - h) + x * h, zz, r) + (wide(r0[k], *at) + wide(own[k], *at))

    for k in range(n):
        stages[k]["a2"].wait_recv()
        stages[k]["b2"].wait_recv()

        def third(i, r, k=k):
            to = (z + 1 + i) % 4
            h, zz = to // 2, to % 2
            r2[k][h, zz, r] = so_far(k, h, zz, r).astype(BF)

        rows(k, 3, third)
        for d in (1, 2, 3):
            to = (z + d) % 4
            stages[k]["z", d] = go(remote(k, 4 + d, r2[k].at[to // 2, to % 2], r3[k].at[d - 1], pz[d - 1]))

    for k in range(n):
        (height, _), t, layer = CHUNKS[k]
        for d in (1, 2, 3):
            stages[k]["z", d].wait_recv()
        h, zz = z // 2, z % 2
        for at in range(0, height, 16):
            some = min(16, ms[t].shape[1] - at)
            r = pl.ds(at, 16)
            g = so_far(k, h, zz, r) + wide(r3[k], 0, r) + wide(r3[k], 1, r) + wide(r3[k], 2, r)
            g = g.astype(BF).astype(F32)[:some]
            e = pl.ds(at, some)
            m = 0.9 * ms[t][layer, e] + 0.1 * g
            v = 0.95 * vs[t][layer, e] + 0.05 * g * g
            mo[t][layer, e] = m
            vo[t][layer, e] = v
            w = ws[t][layer, e].astype(F32)
            w = w - 0.02 * (m * lax.rsqrt(v + 1e-8) + 0.1 * w)
            if some < 16:
                w = jnp.concatenate([w, jnp.zeros((16 - some, w.shape[1]), F32)], axis=0)
            new[k][r] = w.astype(BF)
        stages[k]["put"] = pltpu.make_async_copy(new[k], outs[k].at[x, y, h, zz, c], local_sem.at[k, 1])
        stages[k]["put"].start()
        for d in (1, 2, 3):
            stages[k]["gz", d] = go(remote(k, 7 + d, new[k], outs[k].at[x, y, h, zz, c], pz[d - 1]))

    def up_one(k):
        stages[k]["put"].wait()
        for d in (1, 2, 3):
            stages[k]["gz", d].wait_recv()
        o = outs[k]
        stages[k]["ga2"] = go(remote(k, 11, o.at[x, y, 0, :, c], o.at[x, y, 0, :, c], py))
        stages[k]["gb2"] = go(remote(k, 12, o.at[x, y, 1, :, c], o.at[x, y, 1, :, c], px))

    def up_two(k):
        o = outs[k]
        stages[k]["ga2"].wait_recv()
        stages[k]["ga1"] = go(remote(k, 13, o.at[x, :, 0, :, c], o.at[x, :, 0, :, c], px))
        stages[k]["gb2"].wait_recv()
        stages[k]["gb1"] = go(remote(k, 14, o.at[:, y, 1, :, c], o.at[:, y, 1, :, c], py))

    def up_three(k):
        o = outs[k]
        stages[k]["ga1"].wait_recv()
        stages[k]["gb1"].wait_recv()
        stages[k]["gc"] = go(remote(k, 15, o.at[:, :, :, :, c], o.at[:, :, :, :, c], core))

    for k in range(n):
        up_one(k)
        if k >= 1:
            up_two(k - 1)
        if k >= 2:
            up_three(k - 2)
    up_two(n - 1)
    up_three(n - 2)
    up_three(n - 1)
    for k in range(n):
        stages[k]["gc"].wait_recv()
    for copy in sent:
        copy.wait_send()


def sum_and_step(grads, ws, ms, vs):
    n = len(CHUNKS)
    anywhere, vmem = pl.BlockSpec(memory_space=pl.ANY), pl.BlockSpec(memory_space=pltpu.VMEM)
    blocks = [jax.ShapeDtypeStruct((2, 2, 2, 2, 2, *shape), BF) for shape, _, _ in CHUNKS]
    grads = [g.reshape(b.shape) for g, b in zip(grads, blocks, strict=True)]

    def held(*lead):
        return [pltpu.VMEM((*lead, *shape), BF) for shape, _, _ in CHUNKS]

    done = pl.pallas_call(
        exchange,
        out_shape=[*blocks, *(jax.ShapeDtypeStruct(t.shape, F32) for t in (*ms, *vs))],
        in_specs=[anywhere] * n + [vmem] * 9,
        out_specs=[anywhere] * n + [vmem] * 6,
        scratch_shapes=[
            *held(2, 2, 2, 2), *held(2, 2, 2, 2), *held(2, 2, 2), *held(2, 2), *held(3), *held(),
            pltpu.SemaphoreType.DMA((n, 2)), pltpu.SemaphoreType.DMA((n, 16)), pltpu.SemaphoreType.DMA((n, 16)),
        ],
        compiler_params=pltpu.CompilerParams(collective_id=0, has_side_effects=True, vmem_limit_bytes=67043328),
    )(*grads, *ws, *ms, *vs)
    return done[:n], done[n : n + 3], done[n + 3 :]


def solution(mesh):
    def step(x, dy, wg, wu, wd, mg, mu, md, vg, vu, vd):
        grads = gradients(x[0], dy[0], wg, wu, wd)
        me = lax.axis_index("dp")
        ws = [lax.dynamic_slice_in_dim(w, me * rows, rows, 1) for w, rows in ((wg, 28), (wu, 28), (wd, 80))]
        new, m, v = sum_and_step(grads, ws, (mg, mu, md), (vg, vu, vd))
        d1, g1, u1, d0, g0, u0 = new

        def packed(a, b):
            return jnp.stack([t.reshape(32, 32, 2560)[:, :28].reshape(896, 2560) for t in (a, b)])

        down = jnp.stack([t.reshape(2560, 896) for t in (d0, d1)])
        return (packed(g0, g1), packed(u0, u1), down, *m, *v)

    rows = P(None, "dp", None)
    return jax.shard_map(
        step,
        mesh=mesh,
        in_specs=(P(("rep", "dp")), P(("rep", "dp")), P(), P(), P(), *[rows] * 6),
        out_specs=(*[P("rep")] * 3, *[P("rep", "dp", None)] * 6),
        check_vma=False,
    )
```

time: 1810 us -> 762 us (0.42)
  waiting for transfers between devices: 823 us -> 0 us
  Pallas kernels: 0 us -> 365 us
  matrix products: 645 us -> 296 us
  starting transfers between devices: 127 us -> 0 us
  other arithmetic: 103 us -> 35.4 us
  local copies, waits for them, and re-layouts: 80.7 us -> 56.8 us
    dot_general x198 -> x0, waiting for transfers between devices: 655 us -> none  [the longest x66 257 us: matmul(): jnp.dot(a, w, preferred_element_type=jnp.float32).astype(jnp.bfloat16)]
    pallas_call x0 -> x1, Pallas kernels: none -> 365 us  [sum_and_step(): pl.pallas_call(exchange, out_shape=[*blocks, *(jax.ShapeDtypeStruct(t.sha...]
    dot_general x105 -> x17, matrix products: 645 us -> 296 us  [dot(): lax.dot_general(a, b, (((ca,), (cb,)), ((), ())), preferred_element_type=...]
    reshape x3 -> x0, waiting for transfers between devices: 168 us -> none  [step(): t.reshape(-1, *t.shape[2:])]
    dot_general x198 -> x0, starting transfers between devices: 127 us -> none  [the longest x66 45.2 us: layer(): gate = jnp.dot(a, w['w_gate'], preferred_element_type=jnp.float32)]
    dot_general x208 -> x0, other arithmetic: 75 us -> none
    unnamed x44 -> x60, local copies, waits for them, and re-layouts: 61 us -> 23.9 us
    another operation x0 -> x4, local copies, waits for them, and re-layouts: none -> 29 us  [packed(): jnp.stack([t.reshape(32, 32, 2560)[:, :28].reshape(896, 2560) for t in (a...]
  transfers between devices with their start and end apart: 201 -> 0, of which waited for: 188 -> 0; matrix products, arithmetic and copies ran while one was open for 37% -> 0% of each run, Pallas kernels for 0% -> 0%
where the time goes in v1:
time: 762 us; the launch traced here: 754 us
  Pallas kernels  365 us (48%)
  matrix products  296 us (39%)
  local copies, waits for them, and re-layouts  56.8 us (7%)
  other arithmetic  35.4 us (5%)
    pallas_call x1, Pallas kernels, sum_and_step(): pl.pallas_call(exchange, out_shape=[*blocks, *(jax.ShapeDtypeStruct(t.sha...  365 us
    dot_general x17, matrix products, dot(): lax.dot_general(a, b, (((ca,), (cb,)), ((), ())), preferred_element_type=...  296 us
    another operation x4, local copies, waits for them, and re-layouts, packed(): jnp.stack([t.reshape(32, 32, 2560)[:, :28].reshape(896, 2560) for t in (a...  29 us
    unnamed x60, local copies, waits for them, and re-layouts  23.9 us
    another operation x2, other arithmetic, packed(): jnp.stack([t.reshape(32, 32, 2560)[:, :28].reshape(896, 2560) for t in (a...  16.4 us

profile of v1, /device:TPU:25, one launch (start us, length us, event | category | flops | bytes accessed | tf_op | source)
XLA Modules:
  0.0 753.9 jit_solution(14780415783661513418)
XLA Ops:
  9.6 18.3 %fusion.44 = f32[2048,2560]{1,0:T(8,128)} fusion(bf16[2,896,2560]{2,1,0:T(8,128)(2,1)} %param.13, bf16[1,2048,896]{2,1,0:T(8,128)(2,1)} %param.11, f32[2048]{0:T(1024)S(1)} %add_rsqrt_fusion.1), kind=kOutput, calls=%fused_computation.59 | convolution fusion | flops 9400745984 | bytes 29237248 | tf_op jit(solution)/shard_map/dot_general | solution.py:16
  27.9 24.5 %multiply_convert_fusion.1 = (bf16[2048,2560]{1,0:T(8,128)(2,1)}, f32[2048,2560]{1,0:T(8,128)}) fusion(f32[2048,2560]{1,0:T(8,128)} %fusion.44, bf16[2,896,2560]{2,1,0:T(8,128)(2,1)} %param.14, bf16[1,2048,896]{2,1,0:T(8,128)(2,1)S(1)} %copy-done.2, f32[2048]{0:T(1024)S(1)} %add_rsqrt_fusion.1), kind=kOutput, calls=%fused_computation.14 | convolution fusion | flops 9432203264 | bytes 60694528 | tf_op jit(solution)/shard_map/dot_general | solution.py:16
  52.4 14.8 %fusion.22 = (f32[2048]{0:T(1024)S(1)}, bf16[2048,896]{0,1:T(8,128)(2,1)S(1)}) fusion(bf16[2048,2560]{1,0:T(8,128)(2,1)} %get-tuple-element.53, bf16[2,2560,896]{2,1,0:T(8,128)(2,1)} %param.15, bf16[1,2048,896]{1,2,0:T(8,128)(2,1)S(1)} %copy-done), kind=kOutput, calls=%fused_computation.37 | convolution fusion | flops 9404413952 | bytes 22421504 | tf_op jit(solution)/shard_map/dot_general | solution.py:16
  67.2 18.5 %fusion.33 = f32[2048,2560]{1,0:T(8,128)} fusion(bf16[2,896,2560]{2,1,0:T(8,128)(2,1)} %param.14, bf16[2048,896]{0,1:T(8,128)(2,1)S(1)} %get-tuple-element.56, f32[2048]{0:T(1024)S(1)} %add_rsqrt_fusion), kind=kOutput, calls=%fused_computation.48 | convolution fusion | flops 9400745984 | bytes 29237248 | tf_op jit(solution)/shard_map/dot_general | solution.py:16
  85.7 16.1 %convolution_convert_fusion.1 = bf16[2048,2560]{1,0:T(8,128)(2,1)} fusion(bf16[2,2560,896]{2,1,0:T(8,128)(2,1)} %param.15, bf16[1,2048,896]{2,1,0:T(8,128)(2,1)S(1)} %copy-done.3), kind=kOutput, calls=%fused_computation.17 | convolution fusion | flops 9400483840 | bytes 18743296 | tf_op jit(solution)/shard_map/dot_general | solution.py:16
  101.8 31.9 %fusion.3 = (bf16[2048,2560]{1,0:T(8,128)(2,1)}, bf16[2048,2560]{1,0:T(8,128)(2,1)}, f32[2048,2560]{1,0:T(8,128)}) fusion(bf16[2048,2560]{1,0:T(8,128)(2,1)} %convolution_convert_fusion.1, f32[2048,2560]{1,0:T(8,128)} %fusion.33, bf16[2,896,2560]{2,1,0:T(8,128)(2,1)} %param.13, bf16[2048,896]{0,1:T(8,128)(2,1)S(1)} %get-tuple-element.56, ...), kind=kOutput, calls=%fused_computation.7 | convolution fusion | flops 9474146304 | bytes 81666048 | tf_op jit(solution)/shard_map/dot_general | solution.py:16
  133.8 21.7 %fusion.29 = bf16[2560,896]{1,0:T(8,128)(2,1)} fusion(f32[2048,2560]{1,0:T(8,128)} %fusion.33, f32[2048,2560]{1,0:T(8,128)} %get-tuple-element.57, bf16[1,2048,896]{2,1,0:T(8,128)(2,1)} %param.12), kind=kOutput, calls=%fused_computation.43 | convolution fusion | flops 9428992000 | bytes 50200576 | tf_op jit(solution)/shard_map/dot_general | solution.py:16
  162.6 13.6 %convolution_convert_fusion.3 = bf16[1024,2560]{1,0:T(8,128)(2,1)} fusion(bf16[2048,1024]{1,0:T(8,128)(2,1)S(1)} %convolution_convert_fusion.6, bf16[2048,2560]{1,0:T(8,128)(2,1)S(1)} %copy-done.17), kind=kOutput, calls=%fused_computation.40 | convolution fusion | flops 10740039680 | bytes 19922944 | tf_op jit(solution)/shard_map/dot_general | solution.py:16
  176.3 15.9 %convolution_convert_fusion.2 = bf16[1024,2560]{1,0:T(8,128)(2,1)} fusion(bf16[2048,1024]{1,0:T(8,128)(2,1)S(1)} %convolution_convert_fusion.6, bf16[2048,2560]{1,0:T(8,128)(2,1)} %get-tuple-element.51), kind=kOutput, calls=%fused_computation.39 | convolution fusion | flops 10740039680 | bytes 19922944 | tf_op jit(solution)/shard_map/dot_general | solution.py:16
  192.2 14.8 %fusion.31 = f32[2048,896]{0,1:T(8,128)} fusion(bf16[2048,2560]{1,0:T(8,128)(2,1)} %get-tuple-element.51, bf16[2,896,2560]{2,1,0:T(8,128)(2,1)S(1)} %bitcast.98), kind=kOutput, calls=%fused_computation.46 | convolution fusion | flops 9395240960 | bytes 22413312 | tf_op jit(solution)/shard_map/dot_general | solution.py:16
  207.0 16.8 %fusion.18 = (f32[2048]{0:T(1024)S(1)}, f32[2048,896]{0,1:T(8,128)}) fusion(bf16[2048,896]{0,1:T(8,128)(2,1)S(1)} %copy-done.5, f32[2048]{0:T(1024)S(1)} %add_rsqrt_fusion, f32[2048,896]{0,1:T(8,128)} %fusion.31, bf16[2048,2560]{1,0:T(8,128)(2,1)} %get-tuple-element.52, bf16[2,896,2560]{2,1,0:T(8,128)(2,1)} %param.13), kind=kOutput, calls=%fused_computation.33 | convolution fusion | flops 9404413952 | bytes 33439744 | tf_op jit(solution)/shard_map/dot_general | solution.py:16
  229.9 7.7 %fusion.59 = bf16[2048,896]{0,1:T(8,128)(2,1)S(1)} fusion(f32[2048,896]{0,1:T(8,128)} %get-tuple-element.59, bf16[2048,896]{0,1:T(8,128)(2,1)} %copy-done.4, bf16[1,2048,896]{1,2,0:T(8,128)(2,1)} %copy.31, f32[2048]{0:T(1024)S(1)} %broadcast_multiply_fusion, f32[2048]{0:T(1024)S(1)} %add_rsqrt_fusion), kind=kLoop, calls=%fused_computation.74 | loop fusion | flops 12845056 | bytes 18366464 | tf_op jit(solution)/shard_map/add | solution.py:51
  237.6 15.5 %convolution_convert_fusion.4 = bf16[2560,896]{1,0:T(8,128)(2,1)} fusion(bf16[2048,2560]{1,0:T(8,128)(2,1)} %get-tuple-element.53, bf16[2048,896]{0,1:T(8,128)(2,1)S(1)} %fusion.59), kind=kOutput, calls=%fused_computation.44 | convolution fusion | flops 9397534720 | bytes 18743296 | tf_op jit(solution)/shard_map/dot_general | solution.py:16
  260.0 13.6 %convolution_convert_fusion = bf16[2048,2560]{1,0:T(8,128)(2,1)} fusion(bf16[2048,896]{0,1:T(8,128)(2,1)S(1)} %fusion.59, bf16[2,2560,896]{2,1,0:T(8,128)(2,1)S(1)} %bitcast.100), kind=kOutput, calls=%fused_computation.16 | convolution fusion | flops 9400483840 | bytes 18743296 | tf_op jit(solution)/shard_map/dot_general | solution.py:16
  273.6 25.2 %fusion.23 = bf16[1024,2560]{1,0:T(8,128)(2,1)} fusion(bf16[2048,1024]{1,0:T(8,128)(2,1)} %convolution_convert_fusion.5, f32[2048,2560]{1,0:T(8,128)} %get-tuple-element.54, bf16[2048,2560]{1,0:T(8,128)(2,1)} %convolution_convert_fusion, f32[2048,2560]{1,0:T(8,128)} %fusion.44), kind=kOutput, calls=%fused_computation.41 | convolution fusion | flops 10797711360 | bytes 61865984 | tf_op jit(solution)/shard_map/dot_general | solution.py:16
  298.9 20.5 %fusion.26 = bf16[1024,2560]{1,0:T(8,128)(2,1)} fusion(bf16[2048,1024]{1,0:T(8,128)(2,1)} %convolution_convert_fusion.5, f32[2048,2560]{1,0:T(8,128)} %fusion.44, bf16[2048,2560]{1,0:T(8,128)(2,1)} %convolution_convert_fusion), kind=kOutput, calls=%fused_computation.42 | convolution fusion | flops 10776739840 | bytes 40894464 | tf_op jit(solution)/shard_map/dot_general | solution.py:16
  327.0 364.7 %shard_map.178 = (bf16[2,2,2,2,2,80,896]{6,5,4,3,2,1,0:T(8,128)(2,1)}, bf16[2,2,2,2,2,32,2560]{6,5,4,3,2,1,0:T(8,128)(2,1)}, bf16[2,2,2,2,2,32,2560]{6,5,4,3,2,1...) custom-call(bf16[2,2,2,2,2,80,896]{6,5,4,3,2,1,0:T(8,128)(2,1)} %bit, ...), custom_call_target="tpu_custom_call" | custom-call | tf_op jit(solution)/shard_map/pallas_call | solution.py:239
  691.8 7.2 stack_reshape.19
  699.0 7.4 stack_reshape.18
  706.4 8.2 %pad_maximum_fusion = bf16[2,896,2560]{2,1,0:T(8,128)(2,1)} fusion(bf16[1,896,2560]{2,1,0:T(8,128)(2,1)} %stack_reshape.19, bf16[1,896,2560]{2,1,0:T(8,128)(2,1)} %stack_reshape.18), kind=kLoop, calls=%fused_computation.21 | loop fusion | flops 4587520 | bytes 18350080 | tf_op jit(solution)/shard_map/stack | solution.py:262
  714.6 7.2 stack_reshape.21
  721.8 7.2 stack_reshape.20
  729.0 8.2 %pad_maximum_fusion.1 = bf16[2,896,2560]{2,1,0:T(8,128)(2,1)} fusion(bf16[1,896,2560]{2,1,0:T(8,128)(2,1)} %stack_reshape.21, bf16[1,896,2560]{2,1,0:T(8,128)(2,1)} %stack_reshape.20), kind=kLoop, calls=%fused_computation.22 | loop fusion | flops 4587520 | bytes 18350080 | tf_op jit(solution)/shard_map/stack | solution.py:262
  737.2 8.4 %pad_maximum_fusion.2 = bf16[2,2560,896]{2,1,0:T(8,128)(2,1)} fusion(bf16[1,2560,896]{2,1,0:T(8,128)(2,1)} %bitcast.93, bf16[1,2560,896]{2,1,0:T(8,128)(2,1)} %bitcast.94), kind=kLoop, calls=%fused_computation.23 | loop fusion | flops 4587520 | bytes 18350080 | tf_op jit(solution)/shard_map/stack | solution.py:264
  (73 shorter events, 44.5 us)
Async XLA Ops:
  9.6 18.3 %copy-start.15 = (f32[2048]{0:T(1024)}, f32[2048]{0:T(1024)S(1)}, u32[]{:S(2)}) copy-start(f32[2048]{0:T(1024)S(1)} %add_rsqrt_fusion.1) | copy-start | bytes 24580
  9.6 18.3 %copy-start.2 = (bf16[1,2048,896]{2,1,0:T(8,128)(2,1)S(1)}, bf16[1,2048,896]{2,1,0:T(8,128)(2,1)}, u32[]{:S(2)}) copy-start(bf16[1,2048,896]{2,1,0:T(8,128)(2,1)} %param.11) | copy-start | bytes 11010052
  27.9 24.5 %copy-start = (bf16[1,2048,896]{1,2,0:T(8,128)(2,1)S(1)}, bf16[1,2048,896]{1,2,0:T(8,128)(2,1)}, u32[]{:S(2)}) copy-start(bf16[1,2048,896]{1,2,0:T(8,128)(2,1)} %copy.30) | copy-start | bytes 11010052
  67.2 34.6 %copy-start.4 = (bf16[2048,896]{0,1:T(8,128)(2,1)}, bf16[2048,896]{0,1:T(8,128)(2,1)S(1)}, u32[]{:S(2)}) copy-start(bf16[2048,896]{0,1:T(8,128)(2,1)S(1)} %get-tuple-element.56) | copy-start | bytes 11010052
  67.2 18.5 %copy-start.3 = (bf16[1,2048,896]{2,1,0:T(8,128)(2,1)S(1)}, bf16[1,2048,896]{2,1,0:T(8,128)(2,1)}, u32[]{:S(2)}) copy-start(bf16[1,2048,896]{2,1,0:T(8,128)(2,1)} %param.12) | copy-start | bytes 11010052
  155.5 7.1 copy-start.17
  162.6 29.5 %slice-start = ((s8[9175040]{0:T(1024)(128)(4,1)}), s8[4194304]{0:T(1024)(128)(4,1)S(1)}, s32[]{:S(2)}) async-start(s8[9175040]{0:T(1024)(128)(4,1)} %bitcast.97), calls=%async_computation | async-start | bytes 8388608
  162.6 29.5 %slice-start.1 = ((s8[9175040]{0:T(1024)(128)(4,1)}), s8[4194304]{0:T(1024)(128)(4,1)S(1)}, s32[]{:S(2)}) async-start(s8[9175040]{0:T(1024)(128)(4,1)} %bitcast.97), calls=%async_computation.1 | async-start | bytes 8388608
  176.3 15.9 %slice-start.2 = ((s8[9175040]{0:T(1024)(128)(4,1)}), s8[786432]{0:T(1024)(128)(4,1)S(1)}, s32[]{:S(2)}) async-start(s8[9175040]{0:T(1024)(128)(4,1)} %bitcast.97), calls=%async_computation.2 | async-start | bytes 1572864
  192.1 14.8 %copy-start.5 = (bf16[2048,896]{0,1:T(8,128)(2,1)S(1)}, bf16[2048,896]{0,1:T(8,128)(2,1)}, u32[]{:S(2)}) copy-start(bf16[2048,896]{0,1:T(8,128)(2,1)} %copy-done.4) | copy-start | bytes 11010052
  237.6 15.6 %copy-start.1 = (bf16[1,2048,896]{1,2,0:T(8,128)(2,1)S(1)}, bf16[1,2048,896]{1,2,0:T(8,128)(2,1)}, u32[]{:S(2)}) copy-start(bf16[1,2048,896]{1,2,0:T(8,128)(2,1)} %copy.30) | copy-start | bytes 11010052
  237.6 15.6 %copy-start.16 = (f32[2048]{0:T(1024)S(1)}, f32[2048]{0:T(1024)}, u32[]{:S(2)}) copy-start(f32[2048]{0:T(1024)} %copy-done.15) | copy-start | bytes 24580
  237.6 22.5 %slice-start.3 = ((s8[9175040]{0:T(1024)(128)(4,1)}), s8[4194304]{0:T(1024)(128)(4,1)S(1)}, s32[]{:S(2)}) async-start(s8[9175040]{0:T(1024)(128)(4,1)} %bitcast.99), calls=%async_computation.3 | async-start | bytes 8388608
  237.6 22.4 %slice-start.4 = ((s8[9175040]{0:T(1024)(128)(4,1)}), s8[4194304]{0:T(1024)(128)(4,1)S(1)}, s32[]{:S(2)}) async-start(s8[9175040]{0:T(1024)(128)(4,1)} %bitcast.99), calls=%async_computation.4 | async-start | bytes 8388608
  253.2 6.9 slice-start.5
  298.9 24.3 %copy-start.10 = (f32[2,28,2560]{2,0,1:T(2,128)S(1)}, f32[2,28,2560]{2,0,1:T(2,128)}, u32[]{:S(2)}) copy-start(f32[2,28,2560]{2,0,1:T(2,128)} %param.16) | copy-start | bytes 1720324
  298.9 25.2 %copy-start.11 = (f32[2,28,2560]{2,0,1:T(2,128)S(1)}, f32[2,28,2560]{2,0,1:T(2,128)}, u32[]{:S(2)}) copy-start(f32[2,28,2560]{2,0,1:T(2,128)} %param.17) | copy-start | bytes 1720324
  298.9 26.2 %copy-start.12 = (f32[2,28,2560]{2,0,1:T(2,128)S(1)}, f32[2,28,2560]{2,0,1:T(2,128)}, u32[]{:S(2)}) copy-start(f32[2,28,2560]{2,0,1:T(2,128)} %param.19) | copy-start | bytes 1720324
  298.9 27.2 %copy-start.13 = (f32[2,28,2560]{2,0,1:T(2,128)S(1)}, f32[2,28,2560]{2,0,1:T(2,128)}, u32[]{:S(2)}) copy-start(f32[2,28,2560]{2,0,1:T(2,128)} %param.20) | copy-start | bytes 1720324
  737.2 8.4 %copy-start.9 = (f32[2,28,2560]{2,1,0:T(8,128)S(1)}, f32[2,28,2560]{2,1,0:T(8,128)}, u32[]{:S(2)}) copy-start(f32[2,28,2560]{2,1,0:T(8,128)} %get-tuple-element.45) | copy-start | bytes 1720324
  737.2 9.7 %copy-start.8 = (f32[2,28,2560]{2,1,0:T(8,128)S(1)}, f32[2,28,2560]{2,1,0:T(8,128)}, u32[]{:S(2)}) copy-start(f32[2,28,2560]{2,1,0:T(8,128)} %get-tuple-element.46) | copy-start | bytes 1720324
  737.2 10.9 %copy-start.7 = (f32[2,28,2560]{2,1,0:T(8,128)S(1)}, f32[2,28,2560]{2,1,0:T(8,128)}, u32[]{:S(2)}) copy-start(f32[2,28,2560]{2,1,0:T(8,128)} %get-tuple-element.48) | copy-start | bytes 1720324
  737.2 12.2 %copy-start.6 = (f32[2,28,2560]{2,1,0:T(8,128)S(1)}, f32[2,28,2560]{2,1,0:T(8,128)}, u32[]{:S(2)}) copy-start(f32[2,28,2560]{2,1,0:T(8,128)} %get-tuple-element.49) | copy-start | bytes 1720324
  737.2 15.3 %copy-start.14 = (f32[2,80,896]{2,1,0:T(8,128)S(1)}, f32[2,80,896]{2,1,0:T(8,128)}, u32[]{:S(2)}) copy-start(f32[2,80,896]{2,1,0:T(8,128)} %get-tuple-element.85) | copy-start | bytes 1720324

commit v2 on v1

--- a/solution.py
+++ b/solution.py
@@ -23,49 +23,101 @@
 
 
 def spread():
-    f, c = lax.broadcasted_iota(jnp.int32, (896, 1024), 0), lax.broadcasted_iota(jnp.int32, (896, 1024), 1)
-    return (32 * (f // 28) + f % 28 == c).astype(BF)
-
-
-def act_back(dp, g, u):
-    s = jax.nn.sigmoid(g)
-    dp = dp.astype(F32)
-    return (dp * u * (s * (1 + g * (1 - s)))).astype(BF), (dp * g * s).astype(BF)
+    row, f = lax.broadcasted_iota(jnp.int32, (1024, 896), 0), lax.broadcasted_iota(jnp.int32, (1024, 896), 1)
+    block = f // 28
+    return (512 * (block % 2) + 32 * (block // 2) + f % 28 == row).astype(BF)
+
+
+TOKENS, PIECE, COLUMNS = 256, 1280, 256
+
+
+def by_columns(ref, piece, value):
+    for at in range(0, PIECE, COLUMNS):
+        ref[(piece.start + at) // COLUMNS] = value[:, at : at + COLUMNS]
+
+
+def states(x_ref, dy_ref, place_ref, wg_ref, wu_ref, wd_ref, b0_ref, p0_ref, dg0_ref, du0_ref, dh_ref, b1_ref, p1_ref, dg1_ref, du1_ref, by_g, by_u):
+    pieces = [pl.ds(at, PIECE) for at in range(0, 2560, PIECE)]
+    x = x_ref[...]
+    a, _ = normed(x)
+    b0_ref[...] = dot(place_ref[...], a, 1, 1).astype(BF)
+    out = jnp.zeros(x.shape, F32)
+    for piece in pieces:
+        g, u = dot(a, wg_ref[0, :, piece], 1, 0), dot(a, wu_ref[0, :, piece], 1, 0)
+        s = jax.nn.sigmoid(g)
+        by_g[:, piece] = u * (s * (1 + g * (1 - s)))
+        by_u[:, piece] = g * s
+        p = (g * s * u).astype(BF)
+        p0_ref[:, piece] = p
+        out += dot(p, wd_ref[0, piece], 1, 0)
+    h = x + out.astype(BF)
+    a, scale = normed(h)
+    b1_ref[...] = dot(place_ref[...], a, 1, 1).astype(BF)
+    dy = dy_ref[...]
+    da = jnp.zeros(x.shape, F32)
+    for piece in pieces:
+        g, u = dot(a, wg_ref[1, :, piece], 1, 0), dot(a, wu_ref[1, :, piece], 1, 0)
+        dp = dot(dy, wd_ref[1, piece], 1, 1).astype(BF).astype(F32)
+        s = jax.nn.sigmoid(g)
+        p1_ref[:, piece] = (g * s * u).astype(BF)
+        dg = (dp * (u * (s * (1 + g * (1 - s))))).astype(BF)
+        du = (dp * (g * s)).astype(BF)
+        by_columns(dg1_ref, piece, dg)
+        by_columns(du1_ref, piece, du)
+        da += dot(dg, wg_ref[1, :, piece], 1, 1) + dot(du, wu_ref[1, :, piece], 1, 1)
+    unit = h.astype(F32) * scale
+    dh = dy + (scale * (da - unit * jnp.mean(da * unit, -1, keepdims=True))).astype(BF)
+    dh_ref[...] = dh
+    for piece in pieces:
+        dp = dot(dh, wd_ref[0, piece], 1, 1).astype(BF).astype(F32)
+        by_columns(dg0_ref, piece, (dp * by_g[:, piece]).astype(BF))
+        by_columns(du0_ref, piece, (dp * by_u[:, piece]).astype(BF))
 
 
 def gradients(x, dy, wg, wu, wd):
+    n = x.shape[0]
+
+    def block(width):
+        return pl.BlockSpec((TOKENS, width), lambda i: (i, 0))
+
+    def whole(t):
+        return pl.BlockSpec(t.shape, lambda i: (0,) * t.ndim, pipeline_mode=pl.Buffered(1))
+
     place = spread()
-    a0, _ = normed(x)
-    g0, u0 = dot(a0, wg[0], 1, 0), dot(a0, wu[0], 1, 0)
-    p0 = (jax.nn.silu(g0) * u0).astype(BF)
-    h1 = x + dot(p0, wd[0], 1, 0).astype(BF)
-    a1, s1 = normed(h1)
-    g1, u1 = dot(a1, wg[1], 1, 0), dot(a1, wu[1], 1, 0)
-    p1 = (jax.nn.silu(g1) * u1).astype(BF)
-    dwd1 = dot(p1, dy, 0, 0).astype(BF)
-    dg1, du1 = act_back(dot(dy, wd[1], 1, 1).astype(BF), g1, u1)
-    b1 = dot(a1, place, 1, 0).astype(BF)
-    dwg1, dwu1 = dot(b1, dg1, 0, 0).astype(BF), dot(b1, du1, 0, 0).astype(BF)
-    da1 = dot(dg1, wg[1], 1, 1) + dot(du1, wu[1], 1, 1)
-    unit = h1.astype(F32) * s1
-    dh1 = dy + (s1 * (da1 - unit * jnp.mean(da1 * unit, -1, keepdims=True))).astype(BF)
-    dwd0 = dot(p0, dh1, 0, 0).astype(BF)
-    dg0, du0 = act_back(dot(dh1, wd[0], 1, 1).astype(BF), g0, u0)
-    b0 = dot(a0, place, 1, 0).astype(BF)
-    dwg0, dwu0 = dot(b0, dg0, 0, 0).astype(BF), dot(b0, du0, 0, 0).astype(BF)
-    return dwd1, dwg1, dwu1, dwd0, dwg0, dwu0
-
-
-CHUNKS = [(TALL, 2, 1), (WIDE, 0, 1), (WIDE, 1, 1), (TALL, 2, 0), (WIDE, 0, 0), (WIDE, 1, 0)]
+    tall = pl.BlockSpec((1024, TOKENS), lambda i: (0, i))
+    tiles = 2560 // COLUMNS
+    tiled = pl.BlockSpec((tiles, TOKENS, COLUMNS), lambda i: (0, i, 0))
+    wide = [jax.ShapeDtypeStruct((n, 2560), BF), *[jax.ShapeDtypeStruct((tiles, n, COLUMNS), BF)] * 2]
+    spread_out = jax.ShapeDtypeStruct((1024, n), BF)
+    b0, p0, dg0, du0, dh, b1, p1, dg1, du1 = pl.pallas_call(
+        states,
+        grid=(n // TOKENS,),
+        out_shape=[spread_out, *wide, jax.ShapeDtypeStruct((n, 896), BF), spread_out, *wide],
+        in_specs=[block(896), block(896), *map(whole, (place, wg, wu, wd))],
+        out_specs=[tall, block(2560), tiled, tiled, block(896), tall, block(2560), tiled, tiled],
+        scratch_shapes=[pltpu.VMEM((TOKENS, 2560), F32)] * 2,
+        compiler_params=pltpu.CompilerParams(vmem_limit_bytes=67043328),
+        cost_estimate=pl.CostEstimate(flops=92 * 10**9, bytes_accessed=10**8, transcendentals=10**7),
+    )(x, dy, place, wg, wu, wd)
+    downs = [dot(a, b, 0, 0).astype(BF) for a, b in ((p1, dy), (p0, dh))]
+    return downs, [b.reshape(2, 512, n) for b in (b1, b0)], (dg1, du1, dg0, du0)
+
+
+CHUNKS = [(TALL, 2, 1), (TALL, 2, 0), (WIDE, 0, 1), (WIDE, 1, 1), (WIDE, 0, 0), (WIDE, 1, 0)]
+
+
+STARTS = (0, 1, 3, 5, 7, 9)
+SHARES = {(2, 0): (0, 3), (2, 2): (3, 5), (1, 1): (5, 8), (1, 3): (8, 10)}
 
 
 def exchange(*refs):
     n = len(CHUNKS)
-    grads, ws, ms, vs = refs[:n], refs[n : n + 3], refs[n + 3 : n + 6], refs[n + 6 : n + 9]
-    outs, mo, vo = refs[n + 9 : 2 * n + 9], refs[2 * n + 9 : 2 * n + 12], refs[2 * n + 12 : 2 * n + 15]
-    scratch = refs[2 * n + 15 :]
+    downs, lefts, rights, ws, ms, vs = refs[:2], refs[2:4], refs[4:8], refs[8:11], refs[11:14], refs[14:17]
+    result, mo, vo = refs[17:20], refs[20:23], refs[23:26]
+    outs = [result[t].at[layer] for _, t, layer in CHUNKS]
+    scratch = refs[26:]
     own, r0, r1, r2, r3, new = (scratch[i * n : (i + 1) * n] for i in range(6))
-    local_sem, send_sem, recv_sem = scratch[6 * n :]
+    local_sem, send_sem, recv_sem, left, right, stage_out, left_sem, right_sem, stage_sem = scratch[6 * n :]
 
     me = lax.axis_index("dp")
     c, z, y, x = me % 2, (me // 2) % 4, (me // 8) % 2, me // 16
@@ -103,14 +155,66 @@
         return copy
 
     stages = [{} for _ in range(n)]
-    for k in range(n):
-        stages[k]["own"] = pltpu.make_async_copy(grads[k].at[:, :, :, :, c], own[k], local_sem.at[k, 0])
+    for k in range(2):
+        stages[k]["own"] = pltpu.make_async_copy(downs[k].at[:, :, :, :, c], own[k], local_sem.at[k, 0])
         stages[k]["own"].start()
-        stages[k]["core"] = go(remote(k, 0, grads[k].at[:, :, :, :, 1 - c], r0[k], core))
-
-    for k in range(n):
-        stages[k]["own"].wait()
-        stages[k]["core"].wait_recv()
+        stages[k]["core"] = go(remote(k, 0, downs[k].at[:, :, :, :, 1 - c], r0[k], core))
+
+    def left_copy(i):
+        return pltpu.make_async_copy(lefts[i], left, left_sem)
+
+    left_copy(0).start()
+    tiles = 2560 // COLUMNS
+
+    def columns(j):
+        return pl.ds(pl.multiple_of(j * COLUMNS, COLUMNS), COLUMNS)
+
+    def right_copy(k, j):
+        return pltpu.make_async_copy(rights[k - 2].at[j], right.at[j % 3], right_sem.at[j % 3])
+
+    def core_copy(k, j):
+        return pltpu.make_async_remote_copy(
+            src_ref=stage_out.at[j % 2], dst_ref=r0[k].at[:, :, :, :, :, columns(j)],
+            send_sem=stage_sem.at[j % 2], recv_sem=recv_sem.at[k, 0],
+            device_id={"dp": core}, device_id_type=MESH,
+        )
+
+    def multiply(k, begin, end):
+        if begin == 0:
+            if k % 2 == 0:
+                left_copy(k // 2 - 1).wait()
+            right_copy(k, 0).start()
+            right_copy(k, 1).start()
+
+        def tile(j, _):
+            @pl.when(j + 2 < tiles)
+            def _():
+                right_copy(k, j + 2).start()
+
+            right_copy(k, j).wait()
+
+            @pl.when(j >= 2)
+            def _():
+                core_copy(k, j).wait_send()
+
+            b = right[j % 3]
+            stage_out[j % 2] = dot(left[1 - c], b, 1, 0).astype(BF).reshape(2, 2, 2, 2, 32, COLUMNS)
+            core_copy(k, j).start()
+            own[k][:, :, :, :, :, columns(j)] = dot(left[c], b, 1, 0).astype(BF).reshape(2, 2, 2, 2, 32, COLUMNS)
+            return 0
+
+        lax.fori_loop(begin, end, tile, 0)
+        if end < tiles:
+            return
+        for j in (tiles - 2, tiles - 1):
+            core_copy(k, j).wait_send()
+        if k == 3:
+            left_copy(1).start()
+
+    def down_one(k):
+        if k < 2:
+            stages[k]["own"].wait()
+        remote(k, 0, r0[k], r0[k], core).wait_recv()
 
         def first(i, r, k=k):
             q, zz = i // 2, i % 2
@@ -128,7 +232,7 @@
         rows(k, 4, second)
         stages[k]["b1"] = go(remote(k, 2, r0[k].at[:, 1 - y, 1], r1[k].at[1], py))
 
-    for k in range(n):
+    def down_two(k):
         stages[k]["a1"].wait_recv()
 
         def first(zz, r, k=k):
@@ -152,7 +256,7 @@
         at = (x, y, h, zz, r)
         return wide(r2[k], h, zz, r) + wide(r1[k], h, y * (1 - h) + x * h, zz, r) + (wide(r0[k], *at) + wide(own[k], *at))
 
-    for k in range(n):
+    def down_three(k):
         stages[k]["a2"].wait_recv()
         stages[k]["b2"].wait_recv()
 
@@ -166,21 +270,22 @@
             to = (z + d) % 4
             stages[k]["z", d] = go(remote(k, 4 + d, r2[k].at[to // 2, to % 2], r3[k].at[d - 1], pz[d - 1]))
 
-    for k in range(n):
+    def take(k):
         (height, _), t, layer = CHUNKS[k]
         for d in (1, 2, 3):
             stages[k]["z", d].wait_recv()
         h, zz = z // 2, z % 2
         for at in range(0, height, 16):
-            some = min(16, ms[t].shape[1] - at)
+            some = min(16, ws[t].shape[1] - at)
             r = pl.ds(at, 16)
             g = so_far(k, h, zz, r) + wide(r3[k], 0, r) + wide(r3[k], 1, r) + wide(r3[k], 2, r)
             g = g.astype(BF).astype(F32)[:some]
             e = pl.ds(at, some)
-            m = 0.9 * ms[t][layer, e] + 0.1 * g
-            v = 0.95 * vs[t][layer, e] + 0.05 * g * g
-            mo[t][layer, e] = m
-            vo[t][layer, e] = v
+            at_mv = (layer, e) if t == 2 else (e, layer)
+            m = 0.9 * ms[t][at_mv] + 0.1 * g
+            v = 0.95 * vs[t][at_mv] + 0.05 * g * g
+            mo[t][at_mv] = m
+            vo[t][at_mv] = v
             w = ws[t][layer, e].astype(F32)
             w = w - 0.02 * (m * lax.rsqrt(v + 1e-8) + 0.1 * w)
             if some < 16:
@@ -212,57 +317,74 @@
         stages[k]["gb1"].wait_recv()
         stages[k]["gc"] = go(remote(k, 15, o.at[:, :, :, :, c], o.at[:, :, :, :, c], core))
 
-    for k in range(n):
-        up_one(k)
-        if k >= 1:
-            up_two(k - 1)
-        if k >= 2:
-            up_three(k - 2)
-    up_two(n - 1)
-    up_three(n - 2)
-    up_three(n - 1)
-    for k in range(n):
+    def finish(k):
         stages[k]["gc"].wait_recv()
+
+    order = (down_one, down_two, down_three, take, up_one, up_two, up_three, finish)
+    starts = STARTS
+    for now in range(starts[-1] + len(order)):
+        for lag, stage in enumerate(order):
+            for k in range(n):
+                if now - starts[k] == lag:
+                    stage(k)
+            for k in range(2, n):
+                if (starts[k] - now, lag) in SHARES:
+                    multiply(k, *SHARES[starts[k] - now, lag])
     for copy in sent:
         copy.wait_send()
 
 
-def sum_and_step(grads, ws, ms, vs):
+def sum_and_step(downs, lefts, rights, ws, ms, vs):
     n = len(CHUNKS)
     anywhere, vmem = pl.BlockSpec(memory_space=pl.ANY), pl.BlockSpec(memory_space=pltpu.VMEM)
-    blocks = [jax.ShapeDtypeStruct((2, 2, 2, 2, 2, *shape), BF) for shape, _, _ in CHUNKS]
-    grads = [g.reshape(b.shape) for g, b in zip(grads, blocks, strict=True)]
+    results = [jax.ShapeDtypeStruct((2, 2, 2, 2, 2, 2, *shape), BF) for shape in (WIDE, WIDE, TALL)]
+    downs = [g.reshape(2, 2, 2, 2, 2, *TALL) for g in downs]
+    tokens = lefts[0].shape[2]
 
     def held(*lead):
         return [pltpu.VMEM((*lead, *shape), BF) for shape, _, _ in CHUNKS]
 
     done = pl.pallas_call(
         exchange,
-        out_shape=[*blocks, *(jax.ShapeDtypeStruct(t.shape, F32) for t in (*ms, *vs))],
-        in_specs=[anywhere] * n + [vmem] * 9,
-        out_specs=[anywhere] * n + [vmem] * 6,
+        out_shape=[*results, *(jax.ShapeDtypeStruct(t.shape, F32) for t in (*ms, *vs))],
+        in_specs=[anywhere] * 8 + [vmem] * 9,
+        out_specs=[anywhere] * 3 + [vmem] * 6,
         scratch_shapes=[
             *held(2, 2, 2, 2), *held(2, 2, 2, 2), *held(2, 2, 2), *held(2, 2), *held(3), *held(),
             pltpu.SemaphoreType.DMA((n, 2)), pltpu.SemaphoreType.DMA((n, 16)), pltpu.SemaphoreType.DMA((n, 16)),
+            pltpu.VMEM((2, 512, tokens), BF), pltpu.VMEM((3, tokens, COLUMNS), BF), pltpu.VMEM((2, 2, 2, 2, 2, 32, COLUMNS), BF),
+            pltpu.SemaphoreType.DMA, pltpu.SemaphoreType.DMA((3,)), pltpu.SemaphoreType.DMA((2,)),
         ],
         compiler_params=pltpu.CompilerParams(collective_id=0, has_side_effects=True, vmem_limit_bytes=67043328),
-    )(*grads, *ws, *ms, *vs)
-    return done[:n], done[n : n + 3], done[n + 3 :]
+    )(*downs, *lefts, *rights, *ws, *ms, *vs)
+    return done[:3], done[3:6], done[6:]
+
+
+def gather_rows(from_ref, to_ref):
+    for i in range(8):
+        to_ref[0, 28 * i : 28 * i + 28] = from_ref[0, i, :28]
+
+
+def packed(t):
+    return pl.pallas_call(
+        gather_rows,
+        grid=(2, 4),
+        out_shape=jax.ShapeDtypeStruct((2, 896, 2560), BF),
+        in_specs=[pl.BlockSpec((1, 8, 32, 2560), lambda i, j: (i, j, 0, 0))],
+        out_specs=pl.BlockSpec((1, 224, 2560), lambda i, j: (i, j, 0)),
+    )(t.reshape(2, 32, 32, 2560))
 
 
 def solution(mesh):
     def step(x, dy, wg, wu, wd, mg, mu, md, vg, vu, vd):
-        grads = gradients(x[0], dy[0], wg, wu, wd)
+        terms = gradients(x[0], dy[0], wg, wu, wd)
         me = lax.axis_index("dp")
         ws = [lax.dynamic_slice_in_dim(w, me * rows, rows, 1) for w, rows in ((wg, 28), (wu, 28), (wd, 80))]
-        new, m, v = sum_and_step(grads, ws, (mg, mu, md), (vg, vu, vd))
-        d1, g1, u1, d0, g0, u0 = new
-
-        def packed(a, b):
-            return jnp.stack([t.reshape(32, 32, 2560)[:, :28].reshape(896, 2560) for t in (a, b)])
-
-        down = jnp.stack([t.reshape(2560, 896) for t in (d0, d1)])
-        return (packed(g0, g1), packed(u0, u1), down, *m, *v)
+        swap = lambda ts: [*(t.swapaxes(0, 1) for t in ts[:2]), ts[2]]
+        new, m, v = sum_and_step(*terms, ws, swap((mg, mu, md)), swap((vg, vu, vd)))
+        m, v = swap(m), swap(v)
+        gate, up, down = new
+        return (packed(gate), packed(up), down.reshape(2, 2560, 896), *m, *v)
 
     rows = P(None, "dp", None)
     return jax.shard_map(

time: 762 us -> 496 us (0.65)
  matrix products: 296 us -> 29.9 us
  Pallas kernels: 365 us -> 437 us
  local copies, waits for them, and re-layouts: 56.8 us -> 16.8 us
  other arithmetic: 35.4 us -> 1.51 us
    dot_general x17 -> x2, matrix products: 296 us -> 29.9 us  [dot(): lax.dot_general(a, b, (((ca,), (cb,)), ((), ())), preferred_element_type=...]
    pallas_call x1 -> x4, Pallas kernels: 365 us -> 437 us  [the longest x1 288 us: sum_and_step(): pl.pallas_call(exchange, out_shape=[*results, *(jax.ShapeDtypeStruct(t.sh...]
    another operation x4 -> x0, local copies, waits for them, and re-layouts: 29 us -> none  [packed(): jnp.stack([t.reshape(32, 32, 2560)[:, :28].reshape(896, 2560) for t in (a...]
    another operation x3 -> x0, other arithmetic: 24.8 us -> none  [the longest x2 16.4 us: packed(): jnp.stack([t.reshape(32, 32, 2560)[:, :28].reshape(896, 2560) for t in (a...]
    unnamed x60 -> x23, local copies, waits for them, and re-layouts: 23.9 us -> 13 us
    add x2 -> x1, other arithmetic: 7.72 us -> 0.01 us  [spread(): return (512 * (block % 2) + 32 * (block // 2) + f % 28 == row).astype(BF)]
where the time goes in v2:
time: 496 us; the launch traced here: 486 us
  Pallas kernels  437 us (88%)
  matrix products  29.9 us (6%)
  local copies, waits for them, and re-layouts  16.8 us (3%)
    pallas_call x1, Pallas kernels, sum_and_step(): pl.pallas_call(exchange, out_shape=[*results, *(jax.ShapeDtypeStruct(t.sh...  288 us
    pallas_call x1, Pallas kernels, gradients(): pl.pallas_call(states, grid=(n // TOKENS,), out_shape=[spread_out, *wide,...  129 us
    dot_general x2, matrix products, dot(): lax.dot_general(a, b, (((ca,), (cb,)), ((), ())), preferred_element_type=...  29.9 us
    pallas_call x2, Pallas kernels, packed(): pl.pallas_call(gather_rows, grid=(2, 4), out_shape=jax.ShapeDtypeStruct((...  19.6 us
    unnamed x23, local copies, waits for them, and re-layouts  13 us

profile of v2, /device:TPU:25, one launch (start us, length us, event | category | flops | bytes accessed | tf_op | source)
XLA Modules:
  0.0 486.4 jit_solution(7019348327248431497)
XLA Ops:
  0.7 1.7 constant_dynamic-slice_fusion.refs_10_
  2.4 2.1 constant_dynamic-slice_fusion.1
  4.5 1.5 fusion.9.place_ref
  6.0 129.2 %shard_map.178 = (bf16[1024,2048]{1,0:T(8,128)(2,1)}, bf16[2048,2560]{1,0:T(8,128)(2,1)}, bf16[10,2048,256]{2,1,0:T(8,128)(2,1)}, bf16[10,2048,256]{2,1,0:T(8,12...) custom-call(bf16[2048,896]{1,0:T(8,128)(2,1)} %bitcast.37, ...), custom_call_target="tpu_custom_call" | custom-call | flops 92000002048 | bytes 100000000 | tf_op jit(solution)/shard_map/pallas_call | solution.py:92
  135.2 0.0 copy-start.6
  135.2 0.0 copy-start.7
  135.2 17.0 %convolution_convert_fusion.1 = bf16[2560,896]{1,0:T(8,128)(2,1)} fusion(bf16[2048,2560]{1,0:T(8,128)(2,1)} %get-tuple-element.27, bf16[1,2048,896]{2,1,0:T(8,128)(2,1)} %param.12), kind=kOutput, calls=%fused_computation.9 | convolution fusion | flops 9397534720 | bytes 18743296 | tf_op jit(solution)/shard_map/dot_general | solution.py:16
  152.2 0.0 copy-done.6
  152.2 0.0 copy-done.7
  152.2 12.9 %convolution_convert_fusion = bf16[2560,896]{1,0:T(8,128)(2,1)} fusion(bf16[2048,2560]{1,0:T(8,128)(2,1)S(1)} %copy-done.6, bf16[2048,896]{1,0:T(8,128)(2,1)S(1)} %copy-done.7), kind=kOutput, calls=%fused_computation.8 | convolution fusion | flops 9397534720 | bytes 18743296 | tf_op jit(solution)/shard_map/dot_general | solution.py:16
  165.1 288.3 %shard_map.179 = (bf16[2,2,2,2,2,2,32,2560]{7,6,5,4,3,2,1,0:T(8,128)(2,1)}, bf16[2,2,2,2,2,2,32,2560]{7,6,5,4,3,2,1,0:T(8,128)(2,1)}, bf16[2,2,2,2,2,2,80,896]{7...) custom-call(bf16[2,2,2,2,2,80,896]{6,5,4,3,2,1,0:T(8,128)(2,1)} %bit, ...), custom_call_target="tpu_custom_call" | custom-call | tf_op jit(solution)/shard_map/pallas_call | solution.py:347
  453.4 9.8 %shard_map.180 = bf16[2,896,2560]{2,1,0:T(8,128)(2,1)} custom-call(bf16[2,32,32,2560]{3,2,1,0:T(8,128)(2,1)} %bitcast.23), custom_call_target="tpu_custom_call" | custom-call | tf_op jit(solution)/shard_map/pallas_call | solution.py:369
  463.2 9.8 %shard_map.181 = bf16[2,896,2560]{2,1,0:T(8,128)(2,1)} custom-call(bf16[2,32,32,2560]{3,2,1,0:T(8,128)(2,1)} %bitcast.22), custom_call_target="tpu_custom_call" | custom-call | tf_op jit(solution)/shard_map/pallas_call | solution.py:369
  473.0 8.1 %copy.27 = bf16[2,2560,896]{2,1,0:T(8,128)(2,1)} copy(bf16[2,2560,896]{2,1,0:T(8,128)(2,1)} %bitcast.24) | data formatting | bytes 18350080
  481.1 0.0 copy-done.5
  481.1 0.8 copy.28
  481.9 0.0 copy-done.4
  481.9 0.8 copy.29
  482.7 0.0 copy-done.3
  482.7 0.8 copy.30
  483.5 0.8 copy.31
  484.3 0.0 copy-done.1
  484.3 0.8 copy.32
  485.2 0.8 copy.33
  (11 shorter events, 0.0 us)
Async XLA Ops:
  135.2 17.0 %copy-start.6 = (bf16[2048,2560]{1,0:T(8,128)(2,1)S(1)}, bf16[2048,2560]{1,0:T(8,128)(2,1)}, u32[]{:S(2)}) copy-start(bf16[2048,2560]{1,0:T(8,128)(2,1)} %get-tuple-element.28) | copy-start | bytes 31457284
  135.2 17.0 %copy-start.7 = (bf16[2048,896]{1,0:T(8,128)(2,1)S(1)}, bf16[2048,896]{1,0:T(8,128)(2,1)}, u32[]{:S(2)}) copy-start(bf16[2048,896]{1,0:T(8,128)(2,1)} %get-tuple-element.29) | copy-start | bytes 11010052
  473.0 8.1 %copy-start.5 = (f32[28,2,2560]{2,1,0:T(2,128)S(1)}, f32[28,2,2560]{2,1,0:T(2,128)}, u32[]{:S(2)}) copy-start(f32[28,2,2560]{2,1,0:T(2,128)} %get-tuple-element.39) | copy-start | bytes 1720324
  473.0 8.9 %copy-start.4 = (f32[28,2,2560]{2,1,0:T(2,128)S(1)}, f32[28,2,2560]{2,1,0:T(2,128)}, u32[]{:S(2)}) copy-start(f32[28,2,2560]{2,1,0:T(2,128)} %get-tuple-element.40) | copy-start | bytes 1720324
  473.0 9.8 %copy-start.3 = (f32[2,80,896]{2,1,0:T(8,128)S(1)}, f32[2,80,896]{2,1,0:T(8,128)}, u32[]{:S(2)}) copy-start(f32[2,80,896]{2,1,0:T(8,128)} %get-tuple-element.67) | copy-start | bytes 1720324
  481.1 2.4 copy-start.2
  481.1 3.3 copy-start.1
  481.1 4.1 copy-start

commit v3 on v2

--- a/solution.py
+++ b/solution.py
@@ -28,7 +28,7 @@
     return (512 * (block % 2) + 32 * (block // 2) + f % 28 == row).astype(BF)
 
 
-TOKENS, PIECE, COLUMNS = 256, 1280, 256
+TOKENS, PIECE, COLUMNS = 256, 2560, 256
 
 
 def by_columns(ref, piece, value):
@@ -136,10 +136,12 @@
         )
 
     def rows(k, blocks, body):
-        per = CHUNKS[k][0][0] // 16
+        height = CHUNKS[k][0][0]
+        some = 32 if height == 32 else 80
+        per = height // some
 
         def step(i, _):
-            body(i // per, pl.ds(pl.multiple_of(i % per * 16, 16), 16))
+            body(i // per, pl.ds(pl.multiple_of(i % per * some, 16), some))
             return 0
 
         lax.fori_loop(0, blocks * per, step, 0)

time: 496 us -> 493 us (level)
  no operation moved by 1% of the time
where the time goes in v3:
time: 493 us; the launch traced here: 483 us
  Pallas kernels  434 us (88%)
  matrix products  29.7 us (6%)
  local copies, waits for them, and re-layouts  16.8 us (3%)
    pallas_call x1, Pallas kernels, sum_and_step(): pl.pallas_call(exchange, out_shape=[*results, *(jax.ShapeDtypeStruct(t.sh...  286 us
    pallas_call x1, Pallas kernels, gradients(): pl.pallas_call(states, grid=(n // TOKENS,), out_shape=[spread_out, *wide,...  128 us
    dot_general x2, matrix products, dot(): lax.dot_general(a, b, (((ca,), (cb,)), ((), ())), preferred_element_type=...  29.7 us
    pallas_call x2, Pallas kernels, packed(): pl.pallas_call(gather_rows, grid=(2, 4), out_shape=jax.ShapeDtypeStruct((...  19.6 us
    unnamed x23, local copies, waits for them, and re-layouts  13 us

profile of v3, /device:TPU:25, one launch (start us, length us, event | category | flops | bytes accessed | tf_op | source)
XLA Modules:
  0.0 483.4 jit_solution(5018428521077357338)
XLA Ops:
  0.7 1.7 constant_dynamic-slice_fusion.refs_10_
  2.4 2.1 constant_dynamic-slice_fusion.1
  4.5 1.5 fusion.9.place_ref
  6.0 128.2 %shard_map.178 = (bf16[1024,2048]{1,0:T(8,128)(2,1)}, bf16[2048,2560]{1,0:T(8,128)(2,1)}, bf16[10,2048,256]{2,1,0:T(8,128)(2,1)}, bf16[10,2048,256]{2,1,0:T(8,12...) custom-call(bf16[2048,896]{1,0:T(8,128)(2,1)} %bitcast.37, ...), custom_call_target="tpu_custom_call" | custom-call | flops 92000002048 | bytes 100000000 | tf_op jit(solution)/shard_map/pallas_call | solution.py:92
  134.2 0.0 copy-start.6
  134.2 0.0 copy-start.7
  134.2 16.8 %convolution_convert_fusion.1 = bf16[2560,896]{1,0:T(8,128)(2,1)} fusion(bf16[2048,2560]{1,0:T(8,128)(2,1)} %get-tuple-element.27, bf16[1,2048,896]{2,1,0:T(8,128)(2,1)} %param.12), kind=kOutput, calls=%fused_computation.9 | convolution fusion | flops 9397534720 | bytes 18743296 | tf_op jit(solution)/shard_map/dot_general | solution.py:16
  151.0 0.0 copy-done.6
  151.0 0.0 copy-done.7
  151.0 12.9 %convolution_convert_fusion = bf16[2560,896]{1,0:T(8,128)(2,1)} fusion(bf16[2048,2560]{1,0:T(8,128)(2,1)S(1)} %copy-done.6, bf16[2048,896]{1,0:T(8,128)(2,1)S(1)} %copy-done.7), kind=kOutput, calls=%fused_computation.8 | convolution fusion | flops 9397534720 | bytes 18743296 | tf_op jit(solution)/shard_map/dot_general | solution.py:16
  164.0 286.4 %shard_map.179 = (bf16[2,2,2,2,2,2,32,2560]{7,6,5,4,3,2,1,0:T(8,128)(2,1)}, bf16[2,2,2,2,2,2,32,2560]{7,6,5,4,3,2,1,0:T(8,128)(2,1)}, bf16[2,2,2,2,2,2,80,896]{7...) custom-call(bf16[2,2,2,2,2,80,896]{6,5,4,3,2,1,0:T(8,128)(2,1)} %bit, ...), custom_call_target="tpu_custom_call" | custom-call | tf_op jit(solution)/shard_map/pallas_call | solution.py:349
  450.4 9.8 %shard_map.180 = bf16[2,896,2560]{2,1,0:T(8,128)(2,1)} custom-call(bf16[2,32,32,2560]{3,2,1,0:T(8,128)(2,1)} %bitcast.23), custom_call_target="tpu_custom_call" | custom-call | tf_op jit(solution)/shard_map/pallas_call | solution.py:371
  460.2 9.8 %shard_map.181 = bf16[2,896,2560]{2,1,0:T(8,128)(2,1)} custom-call(bf16[2,32,32,2560]{3,2,1,0:T(8,128)(2,1)} %bitcast.22), custom_call_target="tpu_custom_call" | custom-call | tf_op jit(solution)/shard_map/pallas_call | solution.py:371
  470.0 8.1 %copy.27 = bf16[2,2560,896]{2,1,0:T(8,128)(2,1)} copy(bf16[2,2560,896]{2,1,0:T(8,128)(2,1)} %bitcast.24) | data formatting | bytes 18350080
  478.1 0.0 copy-done.5
  478.1 0.8 copy.28
  478.9 0.0 copy-done.4
  478.9 0.8 copy.29
  479.7 0.8 copy.30
  480.5 0.0 copy-done.2
  480.5 0.8 copy.31
  481.4 0.8 copy.32
  482.2 0.0 copy-done
  482.2 0.8 copy.33
  (11 shorter events, 0.0 us)
Async XLA Ops:
  134.2 16.8 %copy-start.6 = (bf16[2048,2560]{1,0:T(8,128)(2,1)S(1)}, bf16[2048,2560]{1,0:T(8,128)(2,1)}, u32[]{:S(2)}) copy-start(bf16[2048,2560]{1,0:T(8,128)(2,1)} %get-tuple-element.28) | copy-start | bytes 31457284
  134.2 16.8 %copy-start.7 = (bf16[2048,896]{1,0:T(8,128)(2,1)S(1)}, bf16[2048,896]{1,0:T(8,128)(2,1)}, u32[]{:S(2)}) copy-start(bf16[2048,896]{1,0:T(8,128)(2,1)} %get-tuple-element.29) | copy-start | bytes 11010052
  470.0 8.1 %copy-start.5 = (f32[28,2,2560]{2,1,0:T(2,128)S(1)}, f32[28,2,2560]{2,1,0:T(2,128)}, u32[]{:S(2)}) copy-start(f32[28,2,2560]{2,1,0:T(2,128)} %get-tuple-element.39) | copy-start | bytes 1720324
  470.0 8.9 %copy-start.4 = (f32[28,2,2560]{2,1,0:T(2,128)S(1)}, f32[28,2,2560]{2,1,0:T(2,128)}, u32[]{:S(2)}) copy-start(f32[28,2,2560]{2,1,0:T(2,128)} %get-tuple-element.40) | copy-start | bytes 1720324
  470.0 9.8 %copy-start.3 = (f32[2,80,896]{2,1,0:T(8,128)S(1)}, f32[2,80,896]{2,1,0:T(8,128)}, u32[]{:S(2)}) copy-start(f32[2,80,896]{2,1,0:T(8,128)} %get-tuple-element.67) | copy-start | bytes 1720324
  478.1 2.4 copy-start.2
  478.1 3.3 copy-start.1
  478.1 4.1 copy-start
